TPU v7x, 32 devices: a whole 2x2x4 slice. The times are simulated.
32 devices in a mesh: dp: 8 (over z, x), tensor: 4 (over y, core).
Axes of the slice: x: 2, y: 2, z: 4, core: 2. Of those that a mesh axis runs over, the one named last changes fastest.
Arguments:
- hidden_in: bfloat16 [32, 128, 4096], P(('dp', 'tensor')), parts along dimension 0, may hold values from -6 to 6
- norm_gain: float32 [4096], replicated, may hold values from 0.1 to 1.9
- query_weight: bfloat16 [4096, 4096], P(None, 'tensor'), may hold values from -3 to 3
- kv_weight: bfloat16 [4096, 2048], P(None, 'tensor'), may hold values from -3 to 3
- output_weight: bfloat16 [4096, 4096], P('tensor'), may hold values from -0.09375 to 0.09375
Outputs:
- attention_out: bfloat16 [32, 128, 4096], P(('dp', 'tensor')), parts along dimension 0
There are 8 independent parts, one for each index of `dp`. A program takes and returns all parts, laid end to end along the dimension named above; an argument that names none is the same for every part. Nothing has to cross between parts.
All inputs are finite; a program needn't handle non-finite values.
Results may differ from a plain program's by a relative error of at most 0.014.
The roundings to bfloat16 on the way count: a program that leaves them out, or rounds other values in their place, can miss the bound.
Values may be sent and summed in bfloat16 or wider, within the bound.
A program may use at most 128 MiB of HBM per device.

v0:
```python
import math

import jax
import jax.numpy as jnp
from jax import lax
from jax.sharding import PartitionSpec as P

KVH = 8
HD = 128


EPS = 1e-05
THETA = 500000.0


def partner_2(value, axis, bit):
    mask = 2**bit
    pairs = [(source, source ^ mask) for source in range(lax.axis_size(axis))]
    return lax.ppermute(value, axis, pairs)


def rotary(tensor, positions):
    half_width = tensor.shape[-1] // 2
    frequency = THETA ** (-(jnp.arange(half_width, dtype=jnp.float32) * 2.0 / tensor.shape[-1]))
    angles = positions[:, None] * frequency[None, :]
    cosine = jnp.cos(angles)[:, None, :]
    sine_part = jnp.sin(angles)[:, None, :]
    first_half = tensor[..., :half_width]
    second_half = tensor[..., half_width:]
    return jnp.concatenate(
        (
            first_half * cosine - second_half * sine_part,
            second_half * cosine + first_half * sine_part,
        ),
        axis=-1,
    )


def rms_norm(hidden_in, norm_gain):
    wide = hidden_in.astype(jnp.float32)
    mean_square = jnp.mean(wide * wide, axis=-1, keepdims=True)
    return (wide * lax.rsqrt(mean_square + EPS) * norm_gain).astype(jnp.bfloat16)


def attend(queries, keys, values):
    length = queries.shape[1]
    scores = jnp.einsum(
        "bqhgd,bkhd->bhgqk", queries, keys, preferred_element_type=jnp.float32
    ) / math.sqrt(queries.shape[-1])
    causal = jnp.arange(length)[:, None] >= jnp.arange(length)[None, :]
    scores = jnp.where(causal, scores, -1e30)
    highest = jnp.max(scores, axis=-1, keepdims=True)
    exponent = jnp.exp(scores - highest)
    probabilities = (exponent / jnp.sum(exponent, axis=-1, keepdims=True)).astype(jnp.bfloat16)
    mixed = jnp.einsum(
        "bhgqk,bkhd->bqhgd", probabilities, values, preferred_element_type=jnp.float32
    )
    return mixed.astype(jnp.bfloat16)


def join_heads(stacked, axis_dim):
    sharers = max(lax.axis_size("tensor") // KVH, 1)
    position = lax.axis_index("tensor")
    for bit_index in range(sharers.bit_length() - 1):
        partner = partner_2(stacked, "tensor", bit_index)
        keeps_first = position // (1 << bit_index) % 2 == 0
        stacked = jnp.where(
            keeps_first,
            jnp.concatenate((stacked, partner), axis_dim),
            jnp.concatenate((partner, stacked), axis_dim),
        )
    return stacked


def shards(hidden_in, norm_gain, query_weight, kv_weight, output_weight):
    merged_weight = jnp.concatenate((query_weight, kv_weight), axis=1)
    query_cols = query_weight.shape[1]
    normed = rms_norm(hidden_in, norm_gain)
    projected = jnp.einsum(
        "brd,dc->brc",
        lax.all_gather(normed, "tensor", axis=0, tiled=True),
        merged_weight,
        preferred_element_type=jnp.float32,
    )
    batch, length = (projected.shape[0], projected.shape[1])
    queries_raw = projected[..., :query_cols]
    kv_raw = projected[..., query_cols:].astype(jnp.bfloat16)
    kv_raw = join_heads(kv_raw, 2)
    kv_heads = kv_raw.shape[-1] // (2 * HD)
    kv_split = kv_raw.reshape(batch, length, kv_heads, 2, HD)
    keys_raw = kv_split[:, :, :, 0, :]
    values = kv_split[:, :, :, 1, :]
    heads = query_cols // HD
    positions = jnp.arange(length, dtype=jnp.float32)
    queries = rotary(queries_raw.reshape(batch, length, heads, HD), positions).astype(jnp.bfloat16)
    keys = rotary(keys_raw.astype(jnp.float32), positions).astype(jnp.bfloat16)
    mixed = attend(queries.reshape(batch, length, kv_heads, heads // kv_heads, HD), keys, values)
    mixed_rows = mixed.reshape(batch, length, heads * HD)
    partial_out = jnp.einsum(
        "blc,cd->bld", mixed_rows, output_weight, preferred_element_type=jnp.float32
    )
    return lax.psum_scatter(
        partial_out.astype(jnp.bfloat16), "tensor", scatter_dimension=0, tiled=True
    )


def solution(mesh):
    placed = (
        P(("dp", "tensor"), None, None),
        P(),
        P(None, "tensor"),
        P(None, "tensor"),
        P("tensor", None),
    )
    return jax.shard_map(
        shards,
        mesh=mesh,
        in_specs=placed,
        out_specs=P(("dp", "tensor"), None, None),
        check_vma=False,
    )
```

profile of v0, /device:TPU:0, one launch (start us, length us, event | category | flops | bytes accessed | tf_op | source)
XLA Modules:
  0.0 133.2 jit_solution(11468829457427591245)
XLA Ops:
  6.5 0.0 all-gather.2.cloned.1.call-start
  6.5 1.5 %fusion.9 = f32[128]{0:T(128)S(1)} fusion(bf16[1,128,4096]{2,1,0:T(8,128)(2,1)} %param.5), kind=kLoop, calls=%fused_computation.10 | loop fusion | flops 1572736 | bytes 1049088 | tf_op jit(solution)/shard_map/reduce_sum | solution.py:41
  8.1 2.5 %fusion.11 = bf16[1,128,4096]{2,1,0:T(8,128)(2,1)} fusion(bf16[1,128,4096]{2,1,0:T(8,128)(2,1)} %param.5, f32[4096]{0:T(1024)} %param.6, f32[128]{0:T(128)S(1)} %add_rsqrt_fusion), kind=kLoop, calls=%fused_computation.12 | loop fusion | flops 2097152 | bytes 2114048 | tf_op jit(solution)/shard_map/convert_element_type | solution.py:42
  10.6 0.0 all-gather.2.cloned.1.call-update
  10.6 0.0 reduce-scatter.2.cloned.1.call-start
  10.7 0.3 fusion.29
  11.0 37.0 %all-gather.2.cloned.1.call-done = bf16[4,128,4096]{2,1,0:T(8,128)(2,1)} async-done(((bf16[1,128,4096]{2,1,0:T(8,128)(2,1)}), bf16[4,128,4096]{2,1,0:T(8,128)(2,1)}) %all-gather.2.cloned.1.call-update) | async-done | bytes 4194320 | tf_op jit(solution)/shard_map/all_gather | solution.py:81
  48.0 11.0 %fusion.1 = f32[4,128,1536]{2,1,0:T(8,128)S(1)} fusion(bf16[4,128,4096]{2,1,0:T(8,128)(2,1)} %all-gather.2.cloned.1.call-done, bf16[4096,512]{1,0:T(8,128)(2,1)} %param.8, bf16[4096,1024]{1,0:T(8,128)(2,1)} %param.7), kind=kOutput, calls=%fused_computation.2 | convolution fusion | flops 6467616768 | bytes 19922944 | tf_op jit(solution)/shard_map/brd,dc->brc/dot_general | solution.py:79
  59.0 0.0 copy-start
  59.0 1.0 slice.50
  59.9 0.9 copy-done
  60.8 2.0 %reshape.80 = bf16[4,128,2,2,128]{4,3,2,1,0:T(2,128)(2,1)} reshape(bf16[4,128,512]{2,1,0:T(8,128)(2,1)} %slice.50) | data formatting | bytes 1048576 | tf_op jit(solution)/shard_map/reshape | solution.py:90
  62.8 0.0 slice-start
  62.8 2.3 %fusion.38 = (bf16[4,128,2,1,128]{4,3,2,1,0:T(2,128)(2,1)S(1)}, bf16[4,128,2,1,128]{4,3,2,1,0:T(2,128)(2,1)S(1)}) fusion(bf16[4,128,2,2,128]{4,3,2,1,0:T(2,128)(2,1)} %reshape.80), kind=kLoop, calls=%fused_computation.47 | loop fusion | bytes 1048576 | tf_op jit(solution)/shard_map/slice | solution.py:92
  65.1 0.0 slice-done
  65.1 0.5 copy.24
  65.6 0.3 subtract_convert_fusion.1
  65.8 0.7 subtract_convert_fusion
  66.6 0.2 copy.14
  66.8 0.2 copy.15
  67.1 0.4 copy.22
  67.4 2.6 %fusion.39 = (f32[4,2,4,128]{3,2,1,0:T(4,128)S(1)}, f32[4,2,4,128,128]{3,4,2,1,0:T(8,128)}) fusion(pred[128,128]{0,1:T(8,128)(4,1)S(1)} %iota_compare_fusion, bf16[4,128,2,4,64]{4,1,3,2,0:T(8,128)(2,1)S(1)} %bitcast.53, bf16[4,128,2,4,64]{4,1,3,2,0:T(8,128)(2,1)S(1)} %bitcast.52, bf16[4,128,2,64]{3,1,2,0:T(8,128)(2,1)S(1)} %get-tuple-element.8, ...), kind=kOutput, calls=%fused_computation.48 | convolution fusion | flops 138936448 | bytes 3440640 | tf_op jit(solution)/shard_map/sub | solution.py:53
  70.1 2.0 %convolution_convert_fusion = bf16[4,2,128,4,128]{4,2,3,1,0:T(8,128)(2,1)S(1)} fusion(f32[4,2,4,128,128]{3,4,2,1,0:T(8,128)} %get-tuple-element.14, f32[4,2,4,128]{3,2,1,0:T(4,128)S(1)} %get-tuple-element.13, bf16[4,128,2,1,128]{1,4,2,0,3:T(8,128)(2,1)S(1)} %copy.22), kind=kOutput, calls=%fused_computation.19 | convolution fusion | flops 135790592 | bytes 3424256 | tf_op jit(solution)/shard_map/bhgqk,bkhd->bqhgd/dot_general | solution.py:55
  72.1 9.5 %fusion.6 = bf16[4,128,4096]{2,1,0:T(8,128)(2,1)} fusion(bf16[4,128,1024]{1,2,0:T(8,128)(2,1)S(1)} %bitcast.54, bf16[1024,4096]{1,0:T(8,128)(2,1)} %param.9), kind=kOutput, calls=%fused_computation.7 | convolution fusion | flops 4297064448 | bytes 13631488 | tf_op jit(solution)/shard_map/blc,cd->bld/dot_general | solution.py:99
  81.6 0.0 reduce-scatter.2.cloned.1.call-update
  81.6 44.7 %reduce-scatter.2.cloned.1.call-done = bf16[1,128,4096]{2,1,0:T(8,128)(2,1)} async-done(((bf16[4,128,4096]{2,1,0:T(8,128)(2,1)}), bf16[1,128,4096]{2,1,0:T(8,128)(2,1)}) %reduce-scatter.2.cloned.1.call-update) | async-done | bytes 1048592 | tf_op jit(solution)/shard_map/reduce_scatter | solution.py:102
  (4 shorter events, 0.1 us)
Async XLA Ops:
  6.5 41.4 %all-gather.2.cloned.1.call-start = ((), (), s32[]{:S(2)}) async-start(), calls=%async_computation.1 | async-start | bytes 5242880 | tf_op jit(solution)/shard_map/all_gather | solution.py:81
  10.6 115.7 %reduce-scatter.2.cloned.1.call-start = ((), (), s32[]{:S(2)}) async-start(), calls=%async_computation.2 | async-start | bytes 5242880 | tf_op jit(solution)/shard_map/reduce_scatter | solution.py:102
  59.0 1.8 %copy-start = (f32[4,128,1536]{2,1,0:T(8,128)}, f32[4,128,1536]{2,1,0:T(8,128)S(1)}, u32[]{:S(2)}) copy-start(f32[4,128,1536]{2,1,0:T(8,128)S(1)} %fusion.1) | copy-start | bytes 9437188
  62.8 2.3 %slice-start = ((f32[4,128,1536]{2,1,0:T(8,128)}), f32[4,128,1024]{2,1,0:T(8,128)S(1)}, s32[]{:S(2)}) async-start(f32[4,128,1536]{2,1,0:T(8,128)} %copy-done), calls=%async_computation.3 | async-start | bytes 4194304 | tf_op jit(solution)/shard_map/slice | solution.py:86
Sparse Core Ops, SparseCore 0:
  10.7 37.1 all-gather.1
  81.7 44.5 reduce-scatter.1
where the time goes:
time: 133 us
  waiting for transfers between devices  81.7 us (61%)
  matrix products  25.1 us (19%)
  between operations  13.5 us (10%)
  local copies, waits for them, and re-layouts  7.37 us (6%)
  other arithmetic  5.38 us (4%)
    reduce_scatter x1, waiting for transfers between devices, shards(): lax.psum_scatter(partial_out.astype(jnp.bfloat16), 'tensor', scatter_dime...  44.7 us
    all_gather x1, waiting for transfers between devices, shards(): lax.all_gather(normed, 'tensor', axis=0, tiled=True)  37 us
    dot_general x1, matrix products, shards(): jnp.einsum('brd,dc->brc', lax.all_gather(normed, 'tensor', axis=0, tiled=...  11 us
    dot_general x1, matrix products, shards(): jnp.einsum('blc,cd->bld', mixed_rows, output_weight, preferred_element_ty...  9.5 us
  transfers between devices with their start and end apart: 2, of which 2 were waited for; matrix products, arithmetic and copies ran while one was open for 0% of the time, Pallas kernels for 0%

commit v1 on v0

--- a/solution.py
+++ b/solution.py
@@ -1,8 +1,12 @@
+import functools
 import math
 
 import jax
 import jax.numpy as jnp
 from jax import lax
+import numpy as np
+from jax.experimental import pallas as pl
+from jax.experimental.pallas import tpu as pltpu
 from jax.sharding import PartitionSpec as P
 
 KVH = 8
@@ -72,7 +76,7 @@
     return stacked
 
 
-def shards(hidden_in, norm_gain, query_weight, kv_weight, output_weight):
+def general_shards(hidden_in, norm_gain, query_weight, kv_weight, output_weight):
     merged_weight = jnp.concatenate((query_weight, kv_weight), axis=1)
     query_cols = query_weight.shape[1]
     normed = rms_norm(hidden_in, norm_gain)
@@ -104,6 +108,316 @@
     )
 
 
+MESH = pl.DeviceIdType.MESH
+CORES = 2
+HALVES = 2
+LAG = 3
+OUT_TILES = 8
+
+
+def rotary_tables(length):
+    half = HD // 2
+    frequency = np.float32(THETA) ** (-(np.arange(half, dtype=np.float32) * np.float32(2.0 / HD)))
+    angles = np.arange(length, dtype=np.float32)[:, None] * frequency[None, :].astype(np.float32)
+    cosine, sine = np.cos(angles), np.sin(angles)
+    return (
+        np.concatenate((cosine, cosine), axis=1).astype(np.float32),
+        np.concatenate((-sine, sine), axis=1).astype(np.float32),
+    )
+
+
+def block_kernel(
+    dims,
+    hid, gain, wq, wkv, wo, cosine, sine,
+    out,
+    x, xn, w1, w2, qs, ks, vs, mixed_own, mixed_far,
+    give, got, held, summed, landed, own_acc, own_give, own_got, out_buf,
+    x_sem, w1_sem, w2_sem, sib_send, sib_recv, far_send, far_recv, fwd_send, fwd_recv,
+    give_send, give_recv, sum_send, sum_recv, own_send, own_recv, out_sem,
+):
+    length, kvh, group, q_tiles, o_width = dims
+    part = length // HALVES
+    me = lax.axis_index("tensor")
+    sibling = me + 1 - 2 * lax.rem(me, CORES)
+    across = lax.rem(me + CORES, 2 * CORES)
+
+    def local_copy(src, dst, sem):
+        return pltpu.make_async_copy(src, dst, sem)
+
+    def remote(src, dst, send, recv, target):
+        return pltpu.make_async_remote_copy(
+            src_ref=src, dst_ref=dst, send_sem=send, recv_sem=recv,
+            device_id={"tensor": target}, device_id_type=MESH,
+        )
+
+    def w1_copy(t, kv):
+        cols = pl.ds(pl.multiple_of(t * 2 * HD, 2 * HD), 2 * HD)
+        if kv:
+            return local_copy(wkv.at[:, cols], w1.at[t], w1_sem.at[t])
+        return local_copy(wq.at[:, cols], w1.at[kvh + t], w1_sem.at[kvh + t])
+
+    def w2_copy(j):
+        cols = pl.ds(pl.multiple_of(j * o_width, o_width), o_width)
+        return local_copy(wo.at[:, cols], w2.at[j], w2_sem.at[j])
+
+    def far_copy(h):
+        rows = pl.ds(h * part, part)
+        return remote(hid.at[0, rows], x.at[2, rows], far_send.at[h], far_recv.at[h], across)
+
+    def fwd_copy(h):
+        rows = pl.ds(h * part, part)
+        return remote(x.at[2, rows], x.at[3, rows], fwd_send.at[h], fwd_recv.at[h], sibling)
+
+    def give_copy(h, j):
+        return remote(give.at[h, j], got.at[h, j], give_send.at[h, j], give_recv.at[h, j], sibling)
+
+    def sum_copy(h, j):
+        return remote(summed.at[h, j], landed.at[h, j], sum_send.at[h, j], sum_recv.at[h, j], across)
+
+    def own_copy(j):
+        return remote(own_give.at[j], own_got.at[j], own_send.at[j], own_recv.at[j], sibling)
+
+    def out_copy(j):
+        cols = pl.ds(pl.multiple_of(j * o_width, o_width), o_width)
+        return local_copy(out_buf.at[j], out.at[0, :, cols], out_sem.at[j])
+
+    x_copy = local_copy(hid.at[0], x.at[0], x_sem)
+    sib_copy = remote(hid.at[0], x.at[1], sib_send, sib_recv, sibling)
+
+    x_copy.start()
+    for t in range(kvh):
+        w1_copy(t, True).start()
+    for t in range(q_tiles):
+        w1_copy(t, False).start()
+    for j in range(OUT_TILES):
+        w2_copy(j).start()
+
+    barrier = pltpu.get_barrier_semaphore()
+    for target in (sibling, across):
+        pl.semaphore_signal(barrier, inc=1, device_id={"tensor": target}, device_id_type=MESH)
+    pl.semaphore_wait(barrier, 2)
+
+    sib_copy.start()
+    for h in range(HALVES):
+        far_copy(h).start()
+
+    def normalise(slot, row0, rows, dst0):
+        step = 16
+
+        def body(i, carry):
+            at = pl.multiple_of(i * step, step)
+            wide = x[slot, pl.ds(row0 + at, step), :].astype(jnp.float32)
+            mean_square = jnp.mean(wide * wide, axis=-1, keepdims=True)
+            scaled = wide * lax.rsqrt(mean_square + EPS) * gain[...]
+            xn[pl.ds(dst0 + at, step), :] = scaled.astype(jnp.bfloat16)
+            return carry
+
+        lax.fori_loop(0, rows // step, body, 0)
+
+    def rotate(value, row0, rows):
+        c = cosine[row0 : row0 + rows, :]
+        s = sine[row0 : row0 + rows, :]
+        return value * c + pltpu.roll(value, HD // 2, 1) * s
+
+    def project(slot0, row0, rows, first):
+        both = 2 * rows
+
+        def kv_body(g, carry):
+            if first:
+                w1_copy(g, True).wait()
+            raw = jnp.dot(xn[:both, :], w1[g], preferred_element_type=jnp.float32).astype(jnp.bfloat16)
+            for s in range(2):
+                mine = raw[s * rows : (s + 1) * rows]
+                keys = rotate(mine[:, :HD].astype(jnp.float32), row0, rows)
+                ks[slot0 + s, g, row0 : row0 + rows, :] = keys.astype(jnp.bfloat16)
+                vs[slot0 + s, g, row0 : row0 + rows, :] = mine[:, HD:]
+            return carry
+
+        def q_body(t, carry):
+            if first:
+                w1_copy(t, False).wait()
+            raw = jnp.dot(xn[:both, :], w1[kvh + t], preferred_element_type=jnp.float32)
+            for s in range(2):
+                for e in range(2):
+                    value = raw[s * rows : (s + 1) * rows, e * HD : (e + 1) * HD]
+                    qs[s, 2 * t + e, :rows, :] = rotate(value, row0, rows).astype(jnp.bfloat16)
+            return carry
+
+        lax.fori_loop(0, kvh, kv_body, 0)
+        lax.fori_loop(0, q_tiles, q_body, 0)
+
+    def attention(slot0, row0, rows, mixed):
+        seen = row0 + rows
+        for s in range(2):
+            for g in range(kvh):
+                queries = qs[s, g * group : (g + 1) * group, :rows, :].reshape(group * rows, HD)
+                keys = ks[slot0 + s, g, :seen, :]
+                scores = lax.dot_general(
+                    queries, keys, (((1,), (1,)), ((), ())), preferred_element_type=jnp.float32
+                ) * (1.0 / math.sqrt(HD))
+                scores = scores.reshape(group, rows, seen)
+                position = row0 + lax.broadcasted_iota(jnp.int32, (group, rows, seen), 1)
+                key_at = lax.broadcasted_iota(jnp.int32, (group, rows, seen), 2)
+                scores = jnp.where(position >= key_at, scores, -1e30)
+                highest = jnp.max(scores, axis=-1, keepdims=True)
+                exponent = jnp.exp(scores - highest)
+                total = jnp.sum(exponent, axis=-1, keepdims=True)
+                probabilities = (exponent * (1.0 / total)).astype(jnp.bfloat16)
+                result = jnp.dot(
+                    probabilities.reshape(group * rows, seen),
+                    vs[slot0 + s, g, :seen, :],
+                    preferred_element_type=jnp.float32,
+                ).astype(jnp.bfloat16)
+                for e in range(group):
+                    head = g * group + e
+                    mixed[s * rows : (s + 1) * rows, head * HD : (head + 1) * HD] = result[
+                        e * rows : (e + 1) * rows
+                    ]
+
+    x_copy.wait()
+    normalise(0, 0, length, 0)
+    sib_copy.wait_recv()
+    normalise(1, 0, length, length)
+    project(0, 0, length, True)
+    attention(0, 0, length, mixed_own)
+
+    for h in range(HALVES):
+        row0 = h * part
+        far_copy(h).wait_recv()
+        fwd_copy(h).start()
+        normalise(2, row0, part, 0)
+        fwd_copy(h).wait_recv()
+        normalise(3, row0, part, part)
+        project(2, row0, part, False)
+        attention(2, row0, part, mixed_far)
+
+        def far_out(j, carry, h=h):
+            @pl.when(j < OUT_TILES)
+            def _():
+                if h == 0:
+                    w2_copy(j).wait()
+                partial = jnp.dot(mixed_far[...], w2[j], preferred_element_type=jnp.float32)
+                held[j] = partial[:part]
+                give[h, j] = partial[part:].astype(jnp.bfloat16)
+                give_copy(h, j).start()
+
+            @pl.when(j >= LAG)
+            def _():
+                t = j - LAG
+                give_copy(h, t).wait_recv()
+                summed[h, t] = (held[t] + got[h, t].astype(jnp.float32)).astype(jnp.bfloat16)
+                sum_copy(h, t).start()
+
+            return carry
+
+        lax.fori_loop(0, OUT_TILES + LAG, far_out, 0)
+
+    def own_out(j, carry):
+        partial = jnp.dot(mixed_own[...], w2[j], preferred_element_type=jnp.float32)
+        own_acc[j] = partial[:length]
+        own_give[j] = partial[length:].astype(jnp.bfloat16)
+        own_copy(j).start()
+        return carry
+
+    lax.fori_loop(0, OUT_TILES, own_out, 0)
+
+    for h in range(HALVES):
+
+        def finish(j, carry, h=h):
+            rows = pl.ds(h * part, part)
+            if h == 0:
+                own_copy(j).wait_recv()
+            sum_copy(h, j).wait_recv()
+            out_buf[j, rows, :] = (
+                own_acc[j, rows, :] + own_got[j, rows, :].astype(jnp.float32)
+                + landed[h, j].astype(jnp.float32)
+            ).astype(jnp.bfloat16)
+            if h == HALVES - 1:
+                out_copy(j).start()
+            return carry
+
+        lax.fori_loop(0, OUT_TILES, finish, 0)
+
+    def drain(j, carry):
+        out_copy(j).wait()
+        own_copy(j).wait_send()
+        for h in range(HALVES):
+            give_copy(h, j).wait_send()
+            sum_copy(h, j).wait_send()
+        return carry
+
+    lax.fori_loop(0, OUT_TILES, drain, 0)
+    sib_copy.wait_send()
+    for h in range(HALVES):
+        far_copy(h).wait_send()
+        fwd_copy(h).wait_send()
+
+
+def paired_shards(hidden_in, norm_gain, query_weight, kv_weight, output_weight):
+    _, length, width = hidden_in.shape
+    query_cols, kv_cols = query_weight.shape[1], kv_weight.shape[1]
+    heads, kvh = query_cols // HD, kv_cols // (2 * HD)
+    q_tiles = query_cols // (2 * HD)
+    part = length // HALVES
+    o_width = width // OUT_TILES
+    cosine, sine = rotary_tables(length)
+    bf16, f32 = jnp.bfloat16, jnp.float32
+    dma = pltpu.SemaphoreType.DMA
+    any_spec = pl.BlockSpec(memory_space=pl.ANY)
+    vmem_spec = pl.BlockSpec(memory_space=pltpu.VMEM)
+    dims = (length, kvh, heads // kvh, q_tiles, o_width)
+    return pl.pallas_call(
+        functools.partial(block_kernel, dims),
+        out_shape=jax.ShapeDtypeStruct(hidden_in.shape, bf16),
+        in_specs=[any_spec, vmem_spec, any_spec, any_spec, any_spec, vmem_spec, vmem_spec],
+        out_specs=any_spec,
+        scratch_shapes=[
+            pltpu.VMEM((4, length, width), bf16),
+            pltpu.VMEM((2 * length, width), bf16),
+            pltpu.VMEM((kvh + q_tiles, width, 2 * HD), bf16),
+            pltpu.VMEM((OUT_TILES, query_cols, o_width), bf16),
+            pltpu.VMEM((2, heads, length, HD), bf16),
+            pltpu.VMEM((4, kvh, length, HD), bf16),
+            pltpu.VMEM((4, kvh, length, HD), bf16),
+            pltpu.VMEM((2 * length, query_cols), bf16),
+            pltpu.VMEM((2 * part, query_cols), bf16),
+            pltpu.VMEM((HALVES, OUT_TILES, part, o_width), bf16),
+            pltpu.VMEM((HALVES, OUT_TILES, part, o_width), bf16),
+            pltpu.VMEM((OUT_TILES, part, o_width), f32),
+            pltpu.VMEM((HALVES, OUT_TILES, part, o_width), bf16),
+            pltpu.VMEM((HALVES, OUT_TILES, part, o_width), bf16),
+            pltpu.VMEM((OUT_TILES, length, o_width), f32),
+            pltpu.VMEM((OUT_TILES, length, o_width), bf16),
+            pltpu.VMEM((OUT_TILES, length, o_width), bf16),
+            pltpu.VMEM((OUT_TILES, length, o_width), bf16),
+            dma,
+            dma((kvh + q_tiles,)),
+            dma((OUT_TILES,)),
+            dma, dma,
+            dma((HALVES,)), dma((HALVES,)),
+            dma((HALVES,)), dma((HALVES,)),
+            dma((HALVES, OUT_TILES)), dma((HALVES, OUT_TILES)),
+            dma((HALVES, OUT_TILES)), dma((HALVES, OUT_TILES)),
+            dma((OUT_TILES,)), dma((OUT_TILES,)),
+            dma((OUT_TILES,)),
+        ],
+        compiler_params=pltpu.CompilerParams(
+            collective_id=0, has_side_effects=True, vmem_limit_bytes=60 * 2**20
+        ),
+    )(
+        hidden_in, norm_gain.reshape(1, width), query_weight, kv_weight, output_weight,
+        jnp.asarray(cosine), jnp.asarray(sine),
+    )
+
+
+def shards(hidden_in, norm_gain, query_weight, kv_weight, output_weight):
+    two_chips = lax.axis_size("tensor") == 2 * CORES
+    whole_heads = kv_weight.shape[1] % (2 * HD) == 0
+    if two_chips and whole_heads and hidden_in.shape[0] == 1:
+        return paired_shards(hidden_in, norm_gain, query_weight, kv_weight, output_weight)
+    return general_shards(hidden_in, norm_gain, query_weight, kv_weight, output_weight)
+
+
 def solution(mesh):
     placed = (
         P(("dp", "tensor"), None, None),

time: 133 us -> 54.6 us (0.41)
  waiting for transfers between devices: 81.7 us -> 0 us
  Pallas kernels: 0 us -> 52.1 us
  matrix products: 25.1 us -> 0 us
  between operations: 13.5 us -> 0.01 us
  other arithmetic: 5.38 us -> 0 us
  local copies, waits for them, and re-layouts: 7.37 us -> 2.29 us
    pallas_call x0 -> x1, Pallas kernels: none -> 52.1 us  [paired_shards(): pl.pallas_call(functools.partial(block_kernel, dims), out_shape=jax.Shape...]
    reduce_scatter x1 -> x0, waiting for transfers between devices: 44.7 us -> none  [shards(): lax.psum_scatter(partial_out.astype(jnp.bfloat16), 'tensor', scatter_dime...]
    all_gather x1 -> x0, waiting for transfers between devices: 37 us -> none  [shards(): lax.all_gather(normed, 'tensor', axis=0, tiled=True)]
    dot_general x3 -> x0, matrix products: 22.5 us -> none  [the longest x1 11 us: shards(): jnp.einsum('brd,dc->brc', lax.all_gather(normed, 'tensor', axis=0, tiled=...]
    slice x4 -> x0, local copies, waits for them, and re-layouts: 3.23 us -> none  [the longest x1 2.27 us: shards(): values = kv_split[:, :, :, 1, :]]
    sub x1 -> x0, matrix products: 2.61 us -> none  [attend(): exponent = jnp.exp(scores - highest)]
    convert_element_type x2 -> x0, other arithmetic: 2.57 us -> none  [the longest x1 2.53 us: rms_norm(): (wide * lax.rsqrt(mean_square + EPS) * norm_gain).astype(jnp.bfloat16)]
    reshape x1 -> x0, local copies, waits for them, and re-layouts: 1.96 us -> none  [shards(): kv_split = kv_raw.reshape(batch, length, kv_heads, 2, HD)]
  transfers between devices with their start and end apart: 2 -> 0, of which waited for: 2 -> 0; matrix products, arithmetic and copies ran while one was open for 0% -> 0% of each run, Pallas kernels for 0% -> 0%
where the time goes in v1:
time: 54.6 us; the launch traced here: 54.4 us
  Pallas kernels  52.1 us (95%)
  local copies, waits for them, and re-layouts  2.29 us (4%)
    pallas_call x1, Pallas kernels, paired_shards(): pl.pallas_call(functools.partial(block_kernel, dims), out_shape=jax.Shape...  52.1 us
    unnamed x1, local copies, waits for them, and re-layouts  2.29 us

profile of v1, /device:TPU:0, one launch (start us, length us, event | category | flops | bytes accessed | tf_op | source)
XLA Modules:
  0.0 54.4 jit_solution(9090284263601873238)
XLA Ops:
  0.0 52.1 %shard_map.73 = bf16[1,128,4096]{2,1,0:T(8,128)(2,1)} custom-call(bf16[1,128,4096]{2,1,0:T(8,128)(2,1)} %hid.1, f32[1,4096]{1,0:T(1,128)} %bitcast.1, bf16[4096,1024]{1,0:T(8,128)(2,1)} %wq.1, bf16[4096,512]{1,0:T(8,128)(2,1)} %wkv.1, bf16[1024,4096]{1,0:T(8,128)(2,1)} %wo.1, f32[128,128]{1,0:T(8,128)} %constant.4.clone.cosine, f32[128,128]{1,0:T(8,128)} %constant.5.clone.sine), custom_call_target="tpu_custom_call" | custom-call | tf_op jit(solution)/shard_map/pallas_call | solution.py:369
  52.1 2.3 %copy.9 = bf16[1,128,4096]{2,1,0:T(8,128)(2,1)} copy(bf16[1,128,4096]{2,1,0:T(8,128)(2,1)} %shard_map.73) | data formatting | bytes 2097152

commit v2 on v1

--- a/solution.py
+++ b/solution.py
@@ -128,12 +128,13 @@
 
 def block_kernel(
     dims,
-    hid, gain, wq, wkv, wo, cosine, sine,
+    hid, gain_in, wq, wkv, wo, cosine_in, sine_in,
     out,
+    gain, cosine, sine,
     x, xn, w1, w2, qs, ks, vs, mixed_own, mixed_far,
-    give, got, held, summed, landed, own_acc, own_give, own_got, out_buf,
+    give, got, held, summed, landed, own_acc, own_give, own_got,
     x_sem, w1_sem, w2_sem, sib_send, sib_recv, far_send, far_recv, fwd_send, fwd_recv,
-    give_send, give_recv, sum_send, sum_recv, own_send, own_recv, out_sem,
+    give_send, give_recv, sum_send, sum_recv, own_send, own_recv, table_sem,
 ):
     length, kvh, group, q_tiles, o_width = dims
     part = length // HALVES
@@ -177,14 +178,20 @@
     def own_copy(j):
         return remote(own_give.at[j], own_got.at[j], own_send.at[j], own_recv.at[j], sibling)
 
-    def out_copy(j):
-        cols = pl.ds(pl.multiple_of(j * o_width, o_width), o_width)
-        return local_copy(out_buf.at[j], out.at[0, :, cols], out_sem.at[j])
-
     x_copy = local_copy(hid.at[0], x.at[0], x_sem)
     sib_copy = remote(hid.at[0], x.at[1], sib_send, sib_recv, sibling)
 
+    tables = [
+        local_copy(src, dst, table_sem.at[i])
+        for i, (src, dst) in enumerate(((gain_in, gain), (cosine_in, cosine), (sine_in, sine)))
+    ]
+    barrier = pltpu.get_barrier_semaphore()
+    for target in (sibling, across):
+        pl.semaphore_signal(barrier, inc=1, device_id={"tensor": target}, device_id_type=MESH)
+
     x_copy.start()
+    for table in tables:
+        table.start()
     for t in range(kvh):
         w1_copy(t, True).start()
     for t in range(q_tiles):
@@ -192,14 +199,10 @@
     for j in range(OUT_TILES):
         w2_copy(j).start()
 
-    barrier = pltpu.get_barrier_semaphore()
-    for target in (sibling, across):
-        pl.semaphore_signal(barrier, inc=1, device_id={"tensor": target}, device_id_type=MESH)
     pl.semaphore_wait(barrier, 2)
-
-    sib_copy.start()
     for h in range(HALVES):
         far_copy(h).start()
+    sib_copy.start()
 
     def normalise(slot, row0, rows, dst0):
         step = 16
@@ -274,6 +277,8 @@
                         e * rows : (e + 1) * rows
                     ]
 
+    for table in tables:
+        table.wait()
     x_copy.wait()
     normalise(0, 0, length, 0)
     sib_copy.wait_recv()
@@ -328,18 +333,16 @@
             if h == 0:
                 own_copy(j).wait_recv()
             sum_copy(h, j).wait_recv()
-            out_buf[j, rows, :] = (
+            cols = pl.ds(pl.multiple_of(j * o_width, o_width), o_width)
+            out[0, rows, cols] = (
                 own_acc[j, rows, :] + own_got[j, rows, :].astype(jnp.float32)
                 + landed[h, j].astype(jnp.float32)
             ).astype(jnp.bfloat16)
-            if h == HALVES - 1:
-                out_copy(j).start()
             return carry
 
         lax.fori_loop(0, OUT_TILES, finish, 0)
 
     def drain(j, carry):
-        out_copy(j).wait()
         own_copy(j).wait_send()
         for h in range(HALVES):
             give_copy(h, j).wait_send()
@@ -364,14 +367,16 @@
     bf16, f32 = jnp.bfloat16, jnp.float32
     dma = pltpu.SemaphoreType.DMA
     any_spec = pl.BlockSpec(memory_space=pl.ANY)
-    vmem_spec = pl.BlockSpec(memory_space=pltpu.VMEM)
     dims = (length, kvh, heads // kvh, q_tiles, o_width)
     return pl.pallas_call(
         functools.partial(block_kernel, dims),
-        out_shape=jax.ShapeDtypeStruct(hidden_in.shape, bf16),
-        in_specs=[any_spec, vmem_spec, any_spec, any_spec, any_spec, vmem_spec, vmem_spec],
-        out_specs=any_spec,
+        out_shape=pltpu.VMEM(hidden_in.shape, bf16),
+        in_specs=[any_spec] * 7,
+        out_specs=pl.BlockSpec(memory_space=pltpu.VMEM),
         scratch_shapes=[
+            pltpu.VMEM((1, width), f32),
+            pltpu.VMEM((length, HD), f32),
+            pltpu.VMEM((length, HD), f32),
             pltpu.VMEM((4, length, width), bf16),
             pltpu.VMEM((2 * length, width), bf16),
             pltpu.VMEM((kvh + q_tiles, width, 2 * HD), bf16),
@@ -389,7 +394,6 @@
             pltpu.VMEM((OUT_TILES, length, o_width), f32),
             pltpu.VMEM((OUT_TILES, length, o_width), bf16),
             pltpu.VMEM((OUT_TILES, length, o_width), bf16),
-            pltpu.VMEM((OUT_TILES, length, o_width), bf16),
             dma,
             dma((kvh + q_tiles,)),
             dma((OUT_TILES,)),
@@ -399,7 +403,7 @@
             dma((HALVES, OUT_TILES)), dma((HALVES, OUT_TILES)),
             dma((HALVES, OUT_TILES)), dma((HALVES, OUT_TILES)),
             dma((OUT_TILES,)), dma((OUT_TILES,)),
-            dma((OUT_TILES,)),
+            dma((3,)),
         ],
         compiler_params=pltpu.CompilerParams(
             collective_id=0, has_side_effects=True, vmem_limit_bytes=60 * 2**20

time: 54.6 us -> 51.7 us (0.947)
  Pallas kernels: 52.1 us -> 50.6 us
  local copies, waits for them, and re-layouts: 2.29 us -> 0.97 us
    pallas_call x1, Pallas kernels: 52.1 us -> 50.6 us  [paired_shards(): pl.pallas_call(functools.partial(block_kernel, dims), out_shape=pltpu.VME...]
    unnamed x1, local copies, waits for them, and re-layouts: 2.29 us -> 0.97 us
where the time goes in v2:
time: 51.7 us; the launch traced here: 51.6 us
  Pallas kernels  50.6 us (98%)
  local copies, waits for them, and re-layouts  0.97 us (2%)
    pallas_call x1, Pallas kernels, paired_shards(): pl.pallas_call(functools.partial(block_kernel, dims), out_shape=pltpu.VME...  50.6 us

profile of v2, /device:TPU:0, one launch (start us, length us, event | category | flops | bytes accessed | tf_op | source)
XLA Modules:
  0.0 51.6 jit_solution(12501634682836245916)
XLA Ops:
  0.0 50.6 %shard_map.73 = bf16[1,128,4096]{2,1,0:T(8,128)(2,1)S(1)} custom-call(bf16[1,128,4096]{2,1,0:T(8,128)(2,1)} %hid.1, f32[1,4096]{1,0:T(1,128)} %bitcast.1, bf16[4096,1024]{1,0:T(8,128)(2,1)} %wq.1, bf16[4096,512]{1,0:T(8,128)(2,1)} %wkv.1, bf16[1024,4096]{1,0:T(8,128)(2,1)} %wo.1, f32[128,128]{1,0:T(8,128)} %constant.4.clone.cosine_in, ...), custom_call_target="tpu_custom_call" | custom-call | tf_op jit(solution)/shard_map/pallas_call | solution.py:371
  50.6 1.0 %copy.9 = bf16[1,128,4096]{2,1,0:T(8,128)(2,1)} copy(bf16[1,128,4096]{2,1,0:T(8,128)(2,1)S(1)} %shard_map.73) | data formatting | bytes 2097152
